TPU v7x, 32 devices: a whole 2x2x4 slice. The times are simulated.
32 devices in a mesh: dp: 8 (over y, x, core), feat: 4 (over z).
Axes of the slice: x: 2, y: 2, z: 4, core: 2. Of those that a mesh axis runs over, the one named last changes fastest.
Arguments:
- hidden_states: bfloat16 [64, 256, 1152], P(('dp', 'feat')), may hold values from -6 to 6
- teacher: bfloat16 [64, 256, 1024], P('dp', None, 'feat'), may hold values from -6 to 6
- proj_in: bfloat16 [2048, 1152], replicated, may hold values from -0.1875 to 0.1875
- bias_in: float32 [2048], replicated, may hold values from -3 to 3
- proj_out: bfloat16 [2048, 1024], replicated, may hold values from -0.125 to 0.125
- bias_out: float32 [1024], replicated, may hold values from -3 to 3
Outputs:
- grad_proj_in: float32 [2048, 1152], P(('dp', 'feat'))
- grad_bias_in: float32 [2048], P(('dp', 'feat'))
- grad_proj_out: float32 [2048, 1024], P(('dp', 'feat'))
- grad_bias_out: float32 [1024], replicated
- grad_hidden: bfloat16 [64, 256, 1152], P(('dp', 'feat'))
- loss: float32 [], replicated
All inputs are finite; a program needn't handle non-finite values.
Results may differ from a plain program's by a relative error of at most 0.0095.
The roundings to bfloat16 on the way count: a program that leaves them out, or rounds other values in their place, can miss the bound.
Values may be sent and summed in bfloat16 or wider, within the bound.
A program may use at most 128 MiB of HBM per device.

v0:
```python
import jax
import jax.numpy as jnp
from jax import lax
from jax.sharding import PartitionSpec as P

epsilon = 1e-06


def on_device(hidden_states, teacher, proj_in, bias_in, proj_out, bias_out):
    samples, seq, width = hidden_states.shape
    channels = proj_out.shape[1]
    rows = hidden_states.reshape(samples * seq, width)
    devices = lax.axis_size("dp") * lax.axis_size("feat")
    scale = 1.0 / float(samples * seq * devices)
    pre = (
        lax.dot_general(rows, proj_in, (((1,), (1,)), ((), ())), preferred_element_type=jnp.float32)
        + bias_in
    )
    act = jax.nn.silu(pre).astype(jnp.bfloat16)
    out = jnp.dot(act, proj_out, preferred_element_type=jnp.float32) + bias_out
    target = (
        lax.all_to_all(teacher, "feat", split_axis=0, concat_axis=2, tiled=True)
        .reshape(samples * seq, channels)
        .astype(jnp.float32)
    )
    zz = jnp.sum(out * out, axis=1)
    yy = jnp.sum(target * target, axis=1)
    zy = jnp.sum(out * target, axis=1)
    norm_z = jnp.sqrt(zz + epsilon)
    norm_y = jnp.sqrt(yy + epsilon)
    cosine = zy / (norm_z * norm_y)
    cot = (
        -(target / (norm_z * norm_y)[:, None] - (cosine / (norm_z * norm_z))[:, None] * out)
    ).astype(jnp.bfloat16)
    loss_part = jnp.sum(cosine)
    bias_out_part = jnp.sum(cot.astype(jnp.float32), axis=0)
    back = lax.dot_general(
        cot, proj_out, (((1,), (1,)), ((), ())), preferred_element_type=jnp.float32
    )
    sig = jax.nn.sigmoid(pre)
    dpre = (back * sig * (1.0 + pre * (1.0 - sig))).astype(jnp.bfloat16)
    grad_hidden = (
        jnp.dot(dpre, proj_in, preferred_element_type=jnp.float32)
        .astype(jnp.bfloat16)
        .reshape(samples, seq, width)
    )
    bias_in_part = jnp.sum(dpre.astype(jnp.float32), axis=0)
    grad_first = lax.psum_scatter(
        lax.dot_general(dpre, rows, (((0,), (0,)), ((), ())), preferred_element_type=jnp.float32),
        ("dp", "feat"),
        scatter_dimension=0,
        tiled=True,
    )
    out_term = lax.dot_general(
        act, cot, (((0,), (0,)), ((), ())), preferred_element_type=jnp.float32
    )
    grad_last, grad_bias_first = (
        lax.psum_scatter(out_term, ("dp", "feat"), scatter_dimension=0, tiled=True),
        lax.psum_scatter(bias_in_part, ("dp", "feat"), scatter_dimension=0, tiled=True),
    )
    bias_out_sum, loss_sum = lax.psum((bias_out_part, loss_part), ("dp", "feat"))
    return (
        grad_first * scale,
        grad_bias_first * scale,
        grad_last * scale,
        bias_out_sum * scale,
        grad_hidden,
        -loss_sum * scale,
    )


def solution(mesh):
    return jax.shard_map(
        on_device,
        mesh=mesh,
        in_specs=(P(("dp", "feat"), None, None), P("dp", None, "feat"), P(), P(), P(), P()),
        out_specs=(
            P(("dp", "feat"), None),
            P(("dp", "feat")),
            P(("dp", "feat"), None),
            P(),
            P(("dp", "feat"), None, None),
            P(),
        ),
        check_vma=False,
    )
```

profile of v0, /device:TPU:0, one launch (start us, length us, event | category | flops | bytes accessed | tf_op | source)
XLA Modules:
  0.0 393.6 jit_solution(4499945873667581662)
XLA Ops:
  7.2 6.5 %all-to-all-start = ((bf16[8,256,256]{2,1,0:T(8,128)(2,1)}), bf16[8,256,256]{2,1,0:T(8,128)(2,1)S(1)}, u32[]{:S(2)}, u32[]{:S(2)}) async-start(bf16[8,256,256]{2,1,0:T(8,128)(2,1)} %param.7), calls=%async_computation | async-start | bytes 2097152 | tf_op jit(solution)/shard_map/all_to_all | solution.py:22
  13.7 6.8 %fusion.4 = f32[512,2048]{1,0:T(8,128)} fusion(bf16[512,1152]{1,0:T(8,128)(2,1)S(1)} %bitcast.21, bf16[2048,1152]{1,0:T(8,128)(2,1)} %param.8), kind=kOutput, calls=%fused_computation.21 | convolution fusion | flops 2415919104 | bytes 10092544 | tf_op jit(solution)/shard_map/dot_general | solution.py:16
  20.5 18.9 %all-to-all-done = bf16[8,256,256]{2,1,0:T(8,128)(2,1)S(1)} async-done(((bf16[8,256,256]{2,1,0:T(8,128)(2,1)}), bf16[8,256,256]{2,1,0:T(8,128)(2,1)S(1)}, u32[]{:S(2)}, u32[]{:S(2)}) %all-to-all-start) | async-done | bytes 1048608 | tf_op jit(solution)/shard_map/all_to_all | solution.py:22
  39.4 0.8 copy.15
  40.2 1.8 copy.18
  42.0 0.3 multiply_reduce_fusion.1
  42.5 6.8 %multiply_reduce_fusion.2 = (f32[512]{0:T(512)S(1)}, f32[512]{0:T(512)S(1)}, f32[512,1024]{1,0:T(8,128)S(1)}) fusion(f32[1024]{0:T(1024)S(1)} %copy-done.2, f32[512,1024]{1,0:T(8,128)} %bitcast.24, bf16[2048,1024]{1,0:T(8,128)(2,1)} %param.10, f32[512,2048]{1,0:T(8,128)} %fusion.4, f32[2048]{0:T(1024)S(1)} %copy-done.4), kind=kOutput, calls=%fused_computation.9 | convolution fusion | flops 2156395520 | bytes 12599296 | tf_op jit(solution)/shard_map/dot_general | solution.py:20
  49.3 0.6 divide_reduce_fusion
  49.9 0.5 convert_reduce_fusion.1
  50.5 1.0 copy-done.3
  51.5 3.3 convert_reduce_fusion
  54.8 1.4 copy-done.5
  56.2 5.3 %fusion.5 = f32[2048,1152]{1,0:T(8,128)} fusion(bf16[512,2048]{1,0:T(8,128)(2,1)S(1)} %get-tuple-element.17, bf16[512,1152]{1,0:T(8,128)(2,1)S(1)} %bitcast.22), kind=kOutput, calls=%fused_computation.22 | convolution fusion | flops 2415919104 | bytes 12713984 | tf_op jit(solution)/shard_map/dot_general | solution.py:49
  61.5 0.0 reduce-scatter.3.cloned.1.call-update
  61.5 0.2 reduce-scatter.5.cloned.1.call-start
  61.8 8.0 %fusion.1 = f32[2048,1024]{1,0:T(8,128)} fusion(bf16[512,1024]{1,0:T(8,128)(2,1)S(1)} %get-tuple-element.14, f32[512,2048]{1,0:T(8,128)} %fusion.4, f32[2048]{0:T(1024)S(1)} %copy-done.4), kind=kOutput, calls=%fused_computation.19 | convolution fusion | flops 2153775104 | bytes 13639680 | tf_op jit(solution)/shard_map/dot_general | solution.py:54
  69.8 38.1 %all-reduce.1 = (f32[2048]{0:T(1024)S(1)}, f32[1024]{0:T(1024)S(1)}, f32[]{:T(128)}) all-reduce(f32[2048]{0:T(1024)S(1)} %get-tuple-element.16, f32[1024]{0:T(1024)S(1)} %get-tuple-element.13, f32[]{:T(128)} %get-tuple-element.11), channel_id=3, replica_groups=mesh['dp'=8,'feat'=4] {'dp','feat'}, use_global_device_ids=true, to_apply=%region_6.7.clone | all-reduce | flops 3073 | bytes 24584
  108.5 0.6 dynamic-slice_multiply_fusion
  109.1 0.6 broadcast_multiply_fusion.2
  109.7 6.9 %convolution_convert_fusion = bf16[512,1152]{1,0:T(8,128)(2,1)} fusion(bf16[512,2048]{1,0:T(8,128)(2,1)} %copy-done.5, bf16[2048,1152]{1,0:T(8,128)(2,1)} %param.8), kind=kOutput, calls=%fused_computation.4 | convolution fusion | flops 2416508928 | bytes 7995392 | tf_op jit(solution)/shard_map/dot_general | solution.py:43
  116.6 80.4 %reduce-scatter.3.cloned.1.call-done = f32[64,1152]{1,0:T(8,128)} async-done(((f32[2048,1152]{1,0:T(8,128)}), f32[64,1152]{1,0:T(8,128)}) %reduce-scatter.3.cloned.1.call-update) | async-done | bytes 294928 | tf_op jit(solution)/shard_map/reduce_scatter | solution.py:48
  197.0 1.7 broadcast_multiply_fusion
  198.7 185.3 %reduce-scatter.5.cloned.1.call-done = f32[64,1024]{1,0:T(8,128)} async-done(((f32[2048,1024]{1,0:T(8,128)}), f32[64,1024]{1,0:T(8,128)}) %reduce-scatter.5.cloned.1.call-update) | async-done | bytes 262160 | tf_op jit(solution)/shard_map/reduce_scatter | solution.py:58
  383.9 1.7 broadcast_multiply_fusion.1
  (19 shorter events, 0.1 us)
Async XLA Ops:
  7.2 6.5 %copy-start = (bf16[2,256,1152]{2,1,0:T(8,128)(2,1)S(1)}, bf16[2,256,1152]{2,1,0:T(8,128)(2,1)}, u32[]{:S(2)}) copy-start(bf16[2,256,1152]{2,1,0:T(8,128)(2,1)} %param.6) | copy-start | bytes 3538948
  7.2 32.2 %all-to-all-start = ((bf16[8,256,256]{2,1,0:T(8,128)(2,1)}), bf16[8,256,256]{2,1,0:T(8,128)(2,1)S(1)}, u32[]{:S(2)}, u32[]{:S(2)}) async-start(bf16[8,256,256]{2,1,0:T(8,128)(2,1)} %param.7), calls=%async_computation | async-start | bytes 2097152 | tf_op jit(solution)/shard_map/all_to_all | solution.py:22
  13.7 183.3 %reduce-scatter.3.cloned.1.call-start = ((), (), s32[]{:S(2)}) async-start(), calls=%async_computation.3 | async-start | bytes 9732096 | tf_op jit(solution)/shard_map/reduce_scatter | solution.py:48
  39.4 3.0 copy-start.2
  39.4 3.1 copy-start.4
  42.5 7.5 %copy-start.1 = (f32[64,8,4,256]{3,1,2,0:T(8,128)S(1)}, f32[64,8,4,256]{3,1,2,0:T(8,128)}, u32[]{:S(2)}) copy-start(f32[64,8,4,256]{3,1,2,0:T(8,128)} %copy.18) | copy-start | bytes 6291460
  42.5 8.0 %copy-start.6 = (f32[512,2048]{1,0:T(8,128)S(1)}, f32[512,2048]{1,0:T(8,128)}, u32[]{:S(2)}) copy-start(f32[512,2048]{1,0:T(8,128)} %fusion.4) | copy-start | bytes 12582916
  49.3 2.2 copy-start.3
  54.8 1.4 copy-start.5
  61.5 322.4 %reduce-scatter.5.cloned.1.call-start = ((), (), s32[]{:S(2)}) async-start(), calls=%async_computation.4 | async-start | bytes 8650752 | tf_op jit(solution)/shard_map/reduce_scatter | solution.py:58
Sparse Core Ops, SparseCore 0:
  61.6 135.2 reduce-scatter.2
  199.3 184.6 reduce-scatter.4
where the time goes:
time: 394 us
  waiting for transfers between devices  285 us (72%)
  blocking collectives  38.1 us (10%)
  matrix products  37.1 us (9%)
  between operations  15.9 us (4%)
  starting transfers between devices  6.71 us (2%)
  other arithmetic  6.08 us (2%)
  local copies, waits for them, and re-layouts  5.03 us (1%)
    reduce_scatter x1, waiting for transfers between devices, on_device(): lax.psum_scatter(out_term, ('dp', 'feat'), scatter_dimension=0, tiled=True)  185 us
    reduce_scatter x1, waiting for transfers between devices, on_device(): lax.psum_scatter(lax.dot_general(dpre, rows, (((0,), (0,)), ((), ())), pr...  80.4 us
    unnamed x1, blocking collectives  38.1 us
    all_to_all x1, waiting for transfers between devices, on_device(): lax.all_to_all(teacher, 'feat', split_axis=0, concat_axis=2, tiled=True)  18.9 us
    dot_general x1, matrix products, on_device(): lax.dot_general(act, cot, (((0,), (0,)), ((), ())), preferred_element_typ...  7.97 us
  transfers between devices with their start and end apart: 3, of which 3 were waited for; matrix products, arithmetic and copies ran while one was open for 6% of the time, Pallas kernels for 0%

commit v1 on v0

v1 whole, which is shorter than its diff:
```python
import functools

import jax
import jax.numpy as jnp
from jax import lax
from jax.experimental import pallas as pl
from jax.experimental.pallas import tpu as pltpu
from jax.sharding import PartitionSpec as P

epsilon = 1e-06
f32 = jnp.float32
bf16 = jnp.bfloat16


def log2(n):
    return n.bit_length() - 1


def stage_orders(dp, feat):
    m, f = log2(dp), log2(feat)
    across = [("dp", b) for b in range(1, m)]
    half = len(across) // 2
    tail = [("feat", b) for b in range(f)]
    first = [("dp", 0)] + across + tail
    second = [("dp", 0)] + across[half:] + across[:half] + tail
    return first, second


def splits(order, dp, feat):
    left = [("dp", b) for b in reversed(range(log2(dp)))] + [("feat", b) for b in reversed(range(log2(feat)))]
    out = []
    for bit in order:
        p = left.index(bit)
        out.append((2**p, 2 ** (len(left) - p - 1)))
        left.remove(bit)
    return out


def grads_kernel(plan, scale, act, cot, dpre, rows, small, gout, gin, gsmall, act_t, dpre_t, *rest):
    streams, dp, feat, blk = plan
    stages = log2(dp) + log2(feat)
    per = 3 * stages
    bufs = [rest[i * per : (i + 1) * per] for i in range(len(streams))]
    small_send, small_recv, send_sem, recv_sem = rest[len(streams) * per :]
    place = {"dp": lax.axis_index("dp"), "feat": lax.axis_index("feat")}

    def mine(bit):
        axis, b = bit
        return lax.rem(lax.div(place[axis], 2**b), 2)

    def partner(bit):
        axis, b = bit
        return {axis: place[axis] + (1 - 2 * mine(bit)) * 2**b}

    barrier = pltpu.get_barrier_semaphore()
    for bit in streams[0][0]:
        pl.semaphore_signal(barrier, inc=1, device_id=partner(bit), device_id_type=pl.DeviceIdType.MESH)
    pl.semaphore_wait(barrier, stages)

    def copy(s, k):
        keep, send, recv = bufs[s][3 * k : 3 * k + 3]
        return pltpu.make_async_remote_copy(
            src_ref=send, dst_ref=recv, send_sem=send_sem.at[s, k], recv_sem=recv_sem.at[s, k],
            device_id=partner(streams[s][0][k]), device_id_type=pl.DeviceIdType.MESH,
        )

    def small_copy(k):
        return pltpu.make_async_remote_copy(
            src_ref=small_send.at[k], dst_ref=small_recv.at[k],
            send_sem=send_sem.at[len(streams), k], recv_sem=recv_sem.at[len(streams), k],
            device_id=partner(streams[0][0][k]), device_id_type=pl.DeviceIdType.MESH,
        )

    def transpose(source, target):
        wide = min(256, source.shape[1])

        def body(j, _):
            at = pl.multiple_of(j * wide, wide)
            target[pl.ds(at, wide), :] = source[:, pl.ds(at, wide)].T
            return 0

        lax.fori_loop(0, source.shape[1] // wide, body, 0)

    def produce(s):
        order, split, which, lo_col, hi_col = streams[s]
        lhs, rhs = (act_t, cot) if which == 0 else (dpre_t, rows)
        hi, lo = split[0]
        keep, send, recv = bufs[s][:3]
        own = mine(order[0])

        def term(h, bit):
            at = pl.multiple_of((h * 2 + bit) * (lo * blk), lo * blk)
            got = jnp.dot(lhs[pl.ds(at, lo * blk), :], rhs[:, lo_col:hi_col], preferred_element_type=f32)
            return got.reshape(lo, blk, hi_col - lo_col)

        def to_send(h, _):
            send[pl.ds(h * lo, lo)] = term(h, 1 - own).astype(bf16)
            return 0

        def to_keep(h, _):
            keep[pl.ds(h * lo, lo)] = term(h, own)
            return 0

        lax.fori_loop(0, hi, to_send, 0)
        copy(s, 0).start()
        lax.fori_loop(0, hi, to_keep, 0)

    def advance(s, k):
        order, split = streams[s][:2]
        hi, lo = split[k]
        keep0, _, recv0 = bufs[s][3 * k - 3 : 3 * k]
        keep, send, recv = bufs[s][3 * k : 3 * k + 3]
        own = mine(order[k])
        copy(s, k - 1).wait_recv()

        def total(i, bit):
            at = (lax.div(i, lo) * 2 + bit) * lo + lax.rem(i, lo)
            return keep0[at] + recv0[at].astype(f32)

        def to_send(i, _):
            send[i] = total(i, 1 - own).astype(bf16)
            return 0

        def to_keep(i, _):
            keep[i] = total(i, own)
            return 0

        lax.fori_loop(0, hi * lo, to_send, 0)
        copy(s, k).start()
        lax.fori_loop(0, hi * lo, to_keep, 0)

    def small_step(k):
        if k == 0:
            small_send[0] = small[...]
        else:
            small_copy(k - 1).wait_recv()
            small_send[k] = small_send[k - 1] + small_recv[k - 1]
        small_copy(k).start()

    def finish(s):
        order, split, which, lo_col, hi_col = streams[s]
        keep, _, recv = bufs[s][3 * stages - 3 :]
        copy(s, stages - 1).wait_recv()
        out = gout if which == 0 else gin
        out[:, lo_col:hi_col] = (keep[0] + recv[0].astype(f32)) * scale

    half = len(streams) // 2
    early, late = range(half), range(half, len(streams))
    transpose(act, act_t)
    for s in early:
        produce(s)
    small_step(0)
    for t in range(1, stages + 2):
        for s in early:
            if t < stages:
                advance(s, t)
            elif t == stages:
                finish(s)
        if t < stages:
            small_step(t)
        if t == 1:
            transpose(dpre, dpre_t)
            for s in late:
                produce(s)
        elif t <= stages:
            for s in late:
                advance(s, t - 1)
        else:
            for s in late:
                finish(s)
    small_copy(stages - 1).wait_recv()
    gsmall[...] = (small_send[stages - 1] + small_recv[stages - 1]) * scale
    for k in range(stages):
        for s in range(len(streams)):
            copy(s, k).wait_send()
        small_copy(k).wait_send()


def reduce_grads(act, cot, dpre, rows, small, scale, dp, feat):
    tokens, hidden = act.shape
    channels, width = cot.shape[1], rows.shape[1]
    blk = hidden // (dp * feat)
    orders = stage_orders(dp, feat)
    stages = log2(dp) + log2(feat)
    streams, bufs = [], []
    for which, size in ((0, channels), (1, width)):
        cut = (size // 2 + 127) // 128 * 128
        for order, lo, hi in ((orders[0], 0, cut), (orders[1], cut, size)):
            split = splits(order, dp, feat)
            streams.append((order, split, which, lo, hi))
            for above, below in split:
                shape = (above * below, blk, hi - lo)
                bufs += [pltpu.VMEM(shape, f32), pltpu.VMEM(shape, bf16), pltpu.VMEM(shape, bf16)]
    vmem = pl.BlockSpec(memory_space=pltpu.VMEM)
    return pl.pallas_call(
        functools.partial(grads_kernel, (streams, dp, feat, blk), scale),
        out_shape=(
            jax.ShapeDtypeStruct((blk, channels), f32),
            jax.ShapeDtypeStruct((blk, width), f32),
            jax.ShapeDtypeStruct(small.shape, f32),
        ),
        in_specs=[vmem] * 5,
        out_specs=(vmem,) * 3,
        scratch_shapes=[pltpu.VMEM((hidden, tokens), bf16), pltpu.VMEM((hidden, tokens), bf16)]
        + bufs
        + [
            pltpu.VMEM((stages,) + small.shape, f32),
            pltpu.VMEM((stages,) + small.shape, f32),
            pltpu.SemaphoreType.DMA((len(streams) + 1, stages)),
            pltpu.SemaphoreType.DMA((len(streams) + 1, stages)),
        ],
        compiler_params=pltpu.CompilerParams(collective_id=0, has_side_effects=True, vmem_limit_bytes=60 * 1024 * 1024),
        name="grads",
    )(act, cot, dpre, rows, small)


def on_device(hidden_states, teacher, proj_in, bias_in, proj_out, bias_out):
    samples, seq, width = hidden_states.shape
    hidden, channels = proj_out.shape
    rows = hidden_states.reshape(samples * seq, width)
    dp, feat = lax.axis_size("dp"), lax.axis_size("feat")
    scale = 1.0 / float(samples * seq * dp * feat)
    target = lax.all_to_all(teacher, "feat", split_axis=0, concat_axis=2, tiled=True)
    target = target.reshape(samples * seq, channels).astype(f32)
    pre = lax.dot_general(rows, proj_in, (((1,), (1,)), ((), ())), preferred_element_type=f32) + bias_in
    act = jax.nn.silu(pre).astype(bf16)
    out = jnp.dot(act, proj_out, preferred_element_type=f32) + bias_out
    zz = jnp.sum(out * out, axis=1)
    yy = jnp.sum(target * target, axis=1)
    zy = jnp.sum(out * target, axis=1)
    norm_z = jnp.sqrt(zz + epsilon)
    norm_y = jnp.sqrt(yy + epsilon)
    cosine = zy / (norm_z * norm_y)
    cot = (-(target / (norm_z * norm_y)[:, None] - (cosine / (norm_z * norm_z))[:, None] * out)).astype(bf16)
    back = lax.dot_general(cot, proj_out, (((1,), (1,)), ((), ())), preferred_element_type=f32)
    sig = jax.nn.sigmoid(pre)
    dpre = (back * sig * (1.0 + pre * (1.0 - sig))).astype(bf16)
    grad_hidden = jnp.dot(dpre, proj_in, preferred_element_type=f32).astype(bf16).reshape(samples, seq, width)
    parts = [jnp.sum(dpre.astype(f32), axis=0), jnp.sum(cot.astype(f32), axis=0), jnp.sum(cosine)[None]]
    count = hidden + channels + 1
    padded = -(-count // 1024) * 1024
    small = jnp.concatenate(parts + [jnp.zeros((padded - count,), f32)]).reshape(padded // 128, 128)
    gout, gin, sums = reduce_grads(act, cot, dpre, rows, small, scale, dp, feat)
    sums = sums.reshape(padded)
    blk = hidden // (dp * feat)
    me = lax.axis_index("dp") * feat + lax.axis_index("feat")
    return (
        gin,
        lax.dynamic_slice(sums, (me * blk,), (blk,)),
        gout,
        sums[hidden : hidden + channels],
        grad_hidden,
        -sums[hidden + channels],
    )


def solution(mesh):
    return jax.shard_map(
        on_device,
        mesh=mesh,
        in_specs=(P(("dp", "feat"), None, None), P("dp", None, "feat"), P(), P(), P(), P()),
        out_specs=(
            P(("dp", "feat"), None),
            P(("dp", "feat")),
            P(("dp", "feat"), None),
            P(),
            P(("dp", "feat"), None, None),
            P(),
        ),
        check_vma=False,
    )
```

time: 394 us -> 129 us (0.33)
  waiting for transfers between devices: 285 us -> 17.1 us
  Pallas kernels: 0 us -> 68.9 us
  blocking collectives: 38.1 us -> 0 us
  matrix products: 37.1 us -> 21.4 us
  between operations: 15.9 us -> 2.58 us
  local copies, waits for them, and re-layouts: 5.03 us -> 10.8 us
  other arithmetic: 6.08 us -> 1.53 us
    reduce_scatter x2 -> x0, waiting for transfers between devices: 266 us -> none  [the longest x1 185 us: on_device(): lax.psum_scatter(out_term, ('dp', 'feat'), scatter_dimension=0, tiled=True)]
    pallas_call x0 -> x1, Pallas kernels: none -> 68.9 us  [reduce_grads(): pl.pallas_call(functools.partial(grads_kernel, (streams, dp, feat, blk),...]
    unnamed x1 -> x0, blocking collectives: 38.1 us -> none
    dot_general x4 -> x2, matrix products: 27 us -> 9.45 us  [the longest x1 5.54 us: on_device(): out = jnp.dot(act, proj_out, preferred_element_type=f32) + bias_out]
    mul x4 -> x0, other arithmetic: 4.55 us -> none  [the longest x1 1.69 us: on_device(): grad_first * scale]
  transfers between devices with their start and end apart: 3 -> 1, of which waited for: 3 -> 1; matrix products, arithmetic and copies ran while one was open for 6% -> 7% of each run, Pallas kernels for 0% -> 0%
where the time goes in v1:
time: 129 us
  Pallas kernels  68.9 us (53%)
  matrix products  21.4 us (17%)
  waiting for transfers between devices  17.1 us (13%)
  local copies, waits for them, and re-layouts  10.8 us (8%)
  starting transfers between devices  6.36 us (5%)
  between operations  2.58 us (2%)
  other arithmetic  1.53 us (1%)
    pallas_call x1, Pallas kernels, reduce_grads(): pl.pallas_call(functools.partial(grads_kernel, (streams, dp, feat, blk),...  68.9 us
    all_to_all x1, waiting for transfers between devices, on_device(): lax.all_to_all(teacher, 'feat', split_axis=0, concat_axis=2, tiled=True)  17.1 us
    dot_general x1, matrix products, on_device(): lax.dot_general(rows, proj_in, (((1,), (1,)), ((), ())), preferred_elemen...  8.62 us
    all_to_all x1, starting transfers between devices, on_device(): lax.all_to_all(teacher, 'feat', split_axis=0, concat_axis=2, tiled=True)  6.36 us
    dot_general x1, matrix products, on_device(): out = jnp.dot(act, proj_out, preferred_element_type=f32) + bias_out  5.54 us
    unnamed x20, local copies, waits for them, and re-layouts  4.96 us
    dot_general x1, matrix products, on_device(): jnp.dot(dpre, proj_in, preferred_element_type=f32).astype(bf16)  3.91 us
    dot_general x1, matrix products, on_device(): lax.dot_general(cot, proj_out, (((1,), (1,)), ((), ())), preferred_elemen...  3.31 us
  transfers between devices with their start and end apart: 1, of which 1 were waited for; matrix products, arithmetic and copies ran while one was open for 7% of the time, Pallas kernels for 0%

profile of v1, /device:TPU:0, one launch (start us, length us, event | category | flops | bytes accessed | tf_op | source)
XLA Modules:
  0.0 128.7 jit_solution(6443313143839115472)
XLA Ops:
  0.6 6.4 %all-to-all-start = ((bf16[8,256,256]{2,1,0:T(8,128)(2,1)}), bf16[8,256,256]{2,1,0:T(8,128)(2,1)S(1)}, u32[]{:S(2)}, u32[]{:S(2)}) async-start(bf16[8,256,256]{2,1,0:T(8,128)(2,1)} %param.7), calls=%async_computation | async-start | bytes 2097152 | tf_op jit(solution)/shard_map/all_to_all | solution.py:223
  7.0 8.6 %multiply_convert_fusion.1 = (bf16[512,2048]{1,0:T(8,128)(2,1)}, f32[512,2048]{1,0:T(8,128)}) fusion(f32[2048]{0:T(1024)} %param.9, bf16[512,1152]{1,0:T(8,128)(2,1)} %bitcast.29, bf16[2048,1152]{1,0:T(8,128)(2,1)} %param.8), kind=kOutput, calls=%fused_computation.2 | convolution fusion | flops 2422210560 | bytes 12197888 | tf_op jit(solution)/shard_map/dot_general | solution.py:225
  15.6 17.1 %all-to-all-done = bf16[8,256,256]{2,1,0:T(8,128)(2,1)S(1)} async-done(((bf16[8,256,256]{2,1,0:T(8,128)(2,1)}), bf16[8,256,256]{2,1,0:T(8,128)(2,1)S(1)}, u32[]{:S(2)}, u32[]{:S(2)}) %all-to-all-start) | async-done | bytes 1048608 | tf_op jit(solution)/shard_map/all_to_all | solution.py:223
  32.7 0.8 copy.14
  33.5 0.5 copy.17
  34.0 0.3 multiply_reduce_fusion.1
  34.4 0.0 copy-done.2
  34.4 0.0 copy-start.5
  34.4 5.5 %multiply_reduce_fusion.2 = (f32[512]{0:T(512)S(1)}, f32[512]{0:T(512)S(1)}, f32[512,1024]{1,0:T(8,128)S(1)}) fusion(f32[1024]{0:T(1024)S(1)} %copy-done.2, f32[512,1024]{1,0:T(8,128)S(1)} %bitcast.26, bf16[512,2048]{1,0:T(8,128)(2,1)} %get-tuple-element.18.act, bf16[2048,1024]{1,0:T(8,128)(2,1)} %param.10), kind=kOutput, calls=%fused_computation.9 | convolution fusion | flops 2150104064 | bytes 10493952 | tf_op jit(solution)/shard_map/dot_general | solution.py:227
  40.0 0.0 copy-start.3
  40.0 0.0 copy-start.4
  40.0 0.6 divide_reduce_fusion
  40.6 0.5 convert_reduce_fusion.1
  41.2 0.0 copy-start
  41.2 1.1 copy-done.3
  42.3 3.3 %convert_reduce_fusion = (f32[2048]{0:T(1024)S(1)}, bf16[512,2048]{1,0:T(8,128)(2,1)S(1)}) fusion(f32[512,2048]{1,0:T(8,128)S(1)} %copy-done.5, f32[2048]{0:T(1024)S(1)} %copy-done.4, bf16[512,1024]{1,0:T(8,128)(2,1)S(1)} %get-tuple-element.17.cot, bf16[2048,1024]{1,0:T(8,128)(2,1)S(1)} %copy-done.3), kind=kOutput, calls=%fused_computation | convolution fusion | flops 2160064512 | bytes 11550720 | tf_op jit(solution)/shard_map/dot_general | solution.py:235
  45.7 3.9 %convolution_convert_fusion = bf16[512,1152]{1,0:T(8,128)(2,1)} fusion(bf16[512,2048]{1,0:T(8,128)(2,1)S(1)} %get-tuple-element.22.dpre, bf16[2048,1152]{1,0:T(8,128)(2,1)S(1)} %bitcast.36), kind=kOutput, calls=%fused_computation.4 | convolution fusion | flops 2416508928 | bytes 7995392 | tf_op jit(solution)/shard_map/dot_general | solution.py:238
  49.6 1.3 %concatenate.3 = f32[4096]{0:T(1024)} concatenate(f32[2048]{0:T(1024)S(1)} %get-tuple-element.21, f32[1024]{0:T(1024)S(1)} %get-tuple-element.16, f32[1]{0:T(128)} %bitcast.3, f32[1023]{0:T(1024)S(1)} %broadcast_in_dim.5), dimensions={0} | concatenate | bytes 32768 | tf_op jit(solution)/shard_map/concatenate | solution.py:242
  50.9 68.9 %grads.1 = (f32[64,1024]{1,0:T(8,128)}, f32[64,1152]{1,0:T(8,128)}, f32[32,128]{1,0:T(8,128)}) custom-call(bf16[512,2048]{1,0:T(8,128)(2,1)} %get-tuple-element.18.act, bf16[512,1024]{1,0:T(8,128)(2,1)} %copy-done, bf16[512,2048]{1,0:T(8,128)(2,1)} %copy-done.1, bf16[512,1152]{1,0:T(8,128)(2,1)} %bitcast.30, f32[32,128]{1,0:T(8,128)} %bitcast.31), custom_call_target="tpu_custom_call" | custom-call | tf_op jit(solution)/shard_map/grads/pallas_call | solution.py:195
  119.8 1.3 slice_bitcast_fusion
  121.1 1.2 slice.12
  122.3 1.3 dynamic_slice.3
  124.2 1.7 %copy.21 = f32[64,1152]{1,0:T(8,128)} copy(f32[64,1152]{1,0:T(8,128)} %get-tuple-element.29) | data formatting | bytes 589824
  125.9 1.7 %copy.22 = f32[64,1024]{1,0:T(8,128)} copy(f32[64,1024]{1,0:T(8,128)} %get-tuple-element.31) | data formatting | bytes 524288
  (17 shorter events, 0.1 us)
Async XLA Ops:
  0.6 32.1 %all-to-all-start = ((bf16[8,256,256]{2,1,0:T(8,128)(2,1)}), bf16[8,256,256]{2,1,0:T(8,128)(2,1)S(1)}, u32[]{:S(2)}, u32[]{:S(2)}) async-start(bf16[8,256,256]{2,1,0:T(8,128)(2,1)} %param.7), calls=%async_computation | async-start | bytes 2097152 | tf_op jit(solution)/shard_map/all_to_all | solution.py:223
  32.7 1.7 %copy-start.2 = (f32[1024]{0:T(1024)S(1)}, f32[1024]{0:T(1024)}, u32[]{:S(2)}) copy-start(f32[1024]{0:T(1024)} %param.11) | copy-start | bytes 12292
  34.4 6.8 %copy-start.5 = (f32[512,2048]{1,0:T(8,128)S(1)}, f32[512,2048]{1,0:T(8,128)}, u32[]{:S(2)}) copy-start(f32[512,2048]{1,0:T(8,128)} %get-tuple-element.19) | copy-start | bytes 12582916
  40.0 2.3 %copy-start.3 = (bf16[2048,1024]{1,0:T(8,128)(2,1)S(1)}, bf16[2048,1024]{1,0:T(8,128)(2,1)}, u32[]{:S(2)}) copy-start(bf16[2048,1024]{1,0:T(8,128)(2,1)} %param.10) | copy-start | bytes 12582916
  40.0 2.3 %copy-start.4 = (f32[2048]{0:T(1024)S(1)}, f32[2048]{0:T(1024)}, u32[]{:S(2)}) copy-start(f32[2048]{0:T(1024)} %param.9) | copy-start | bytes 24580
  40.6 5.0 %slice-start = ((s8[4718592]{0:T(1024)(128)(4,1)}), s8[4194304]{0:T(1024)(128)(4,1)S(1)}, s32[]{:S(2)}) async-start(s8[4718592]{0:T(1024)(128)(4,1)} %bitcast.35), calls=%async_computation.1 | async-start | bytes 8388608
  41.2 4.4 %copy-start = (bf16[512,1024]{1,0:T(8,128)(2,1)}, bf16[512,1024]{1,0:T(8,128)(2,1)S(1)}, u32[]{:S(2)}) copy-start(bf16[512,1024]{1,0:T(8,128)(2,1)S(1)} %get-tuple-element.17.cot) | copy-start | bytes 3145732
  42.3 3.4 %slice-start.1 = ((s8[4718592]{0:T(1024)(128)(4,1)}), s8[524288]{0:T(1024)(128)(4,1)S(1)}, s32[]{:S(2)}) async-start(s8[4718592]{0:T(1024)(128)(4,1)} %bitcast.35), calls=%async_computation.2 | async-start | bytes 1048576
  45.6 3.9 %copy-start.1 = (bf16[512,2048]{1,0:T(8,128)(2,1)}, bf16[512,2048]{1,0:T(8,128)(2,1)S(1)}, u32[]{:S(2)}) copy-start(bf16[512,2048]{1,0:T(8,128)(2,1)S(1)} %get-tuple-element.22.dpre) | copy-start | bytes 6291460

commit v2 on v1

v2 whole, which is shorter than its diff:
```python
import functools

import jax
import jax.numpy as jnp
from jax import lax
from jax.experimental import pallas as pl
from jax.experimental.pallas import tpu as pltpu
from jax.sharding import PartitionSpec as P

epsilon = 1e-06
f32 = jnp.float32
bf16 = jnp.bfloat16
MESH = pl.DeviceIdType.MESH


def log2(n):
    return n.bit_length() - 1


def stage_orders(dp, feat):
    across = [("dp", b) for b in range(1, log2(dp))]
    along = [("feat", b) for b in range(log2(feat))]
    half = len(across) // 2
    core = [("dp", 0)]
    return core + across + along, core + across[half:] + across[:half] + along, core + along + across


def splits(order, dp, feat):
    left = [("dp", b) for b in reversed(range(log2(dp)))] + [("feat", b) for b in reversed(range(log2(feat)))]
    out = []
    for bit in order:
        p = left.index(bit)
        out.append((2**p, 2 ** (len(left) - p - 1)))
        left.remove(bit)
    return out


def train_kernel(plan, teacher_hbm, rows_hbm, win_hbm, wout_hbm, bias_in, bias_out, gout, gin, gsmall, ghid,
                 rows, win, wout, tea, act, act_t, dpre_t, dsilu, out, cot, brow, bacc, lacc, *rest):
    groups, streams, dp, feat, blk = plan
    stages = log2(dp) + log2(feat)
    bufs, at = [], 0
    for _ in streams:
        bufs.append(rest[at : at + 1 + 2 * stages])
        at += 1 + 2 * stages
    small_send, small_recv, send_sem, recv_sem, tea_send, tea_recv, load_sem = rest[at:]
    place = {"dp": lax.axis_index("dp"), "feat": lax.axis_index("feat")}
    dpre = act
    tokens, hidden = act.shape
    channels, width = cot.shape[1], rows.shape[1]
    samples, seq, part = tea.shape[1:]

    def mine(bit):
        axis, b = bit
        return lax.rem(lax.div(place[axis], 2**b), 2)

    def partner(bit):
        axis, b = bit
        return {axis: place[axis] + (1 - 2 * mine(bit)) * 2**b}

    barrier = pltpu.get_barrier_semaphore()
    for b in range(log2(dp)):
        pl.semaphore_signal(barrier, inc=1, device_id=partner(("dp", b)), device_id_type=MESH)
    for r in range(1, feat):
        peer = {"feat": lax.rem(place["feat"] + r, feat)}
        pl.semaphore_signal(barrier, inc=1, device_id=peer, device_id_type=MESH)

    loads = [
        pltpu.make_async_copy(rows_hbm, rows, load_sem.at[0]),
        pltpu.make_async_copy(win_hbm, win, load_sem.at[1]),
        pltpu.make_async_copy(wout_hbm, wout, load_sem.at[2]),
        pltpu.make_async_copy(
            teacher_hbm.at[pl.ds(place["feat"] * samples, samples)], tea.at[place["feat"]], load_sem.at[3]
        ),
    ]
    for load in loads:
        load.start()
    pl.semaphore_wait(barrier, log2(dp) + feat - 1)

    def tea_copy(r):
        peer = lax.rem(place["feat"] + r, feat)
        return pltpu.make_async_remote_copy(
            src_ref=teacher_hbm.at[pl.ds(peer * samples, samples)], dst_ref=tea.at[place["feat"]],
            send_sem=tea_send.at[r - 1], recv_sem=tea_recv.at[r - 1],
            device_id={"feat": peer}, device_id_type=MESH,
        )

    for r in range(1, feat):
        tea_copy(r).start()

    def copy(s, k):
        send, recv = bufs[s][1 + 2 * k : 3 + 2 * k]
        return pltpu.make_async_remote_copy(
            src_ref=send, dst_ref=recv, send_sem=send_sem.at[s, k], recv_sem=recv_sem.at[s, k],
            device_id=partner(streams[s][0][k]), device_id_type=MESH,
        )

    def small_copy(k):
        return pltpu.make_async_remote_copy(
            src_ref=small_send.at[k], dst_ref=small_recv.at[k],
            send_sem=send_sem.at[len(streams), k], recv_sem=recv_sem.at[len(streams), k],
            device_id=partner(streams[0][0][k]), device_id_type=MESH,
        )

    wide = 256

    def first_map(j, _):
        cut = pl.ds(pl.multiple_of(j * wide, wide), wide)
        pre = lax.dot_general(rows[...], win[cut, :], (((1,), (1,)), ((), ())), preferred_element_type=f32)
        pre = pre + bias_in[:, cut]
        sig = jax.nn.sigmoid(pre)
        got = (pre * sig).astype(bf16)
        act[:, cut] = got
        act_t[cut, :] = got.T
        dsilu[:, cut] = sig * (1.0 + pre * (1.0 - sig))
        return 0

    def last_map(j, _):
        cut = pl.ds(pl.multiple_of(j * wide, wide), wide)
        out[:, cut] = jnp.dot(act[...], wout[:, cut], preferred_element_type=f32) + bias_out[:, cut]
        return 0

    some = 64

    def cotangent(i, loss):
        at = pl.ds(pl.multiple_of(i * some, some), some)
        sample, off = lax.div(i, seq // some), lax.rem(i, seq // some)
        inner = pl.ds(pl.multiple_of(off * some, some), some)
        zz = jnp.zeros((some, 1), f32)
        yy, zy = zz, zz
        for c in range(feat):
            o = out[at, c * part : (c + 1) * part]
            t = tea[c, sample, inner, :].astype(f32)
            zz = zz + jnp.sum(o * o, axis=1, keepdims=True)
            yy = yy + jnp.sum(t * t, axis=1, keepdims=True)
            zy = zy + jnp.sum(o * t, axis=1, keepdims=True)
        norm_z = jnp.sqrt(zz + epsilon)
        norm_y = jnp.sqrt(yy + epsilon)
        inverse = 1.0 / (norm_z * norm_y)
        cosine = zy * inverse
        weight = cosine / (norm_z * norm_z)
        for c in range(feat):
            o = out[at, c * part : (c + 1) * part]
            t = tea[c, sample, inner, :].astype(f32)
            got = (weight * o - t * inverse).astype(bf16)
            cot[at, c * part : (c + 1) * part] = got
            bacc[:, c * part : (c + 1) * part] += jnp.sum(got.astype(f32), axis=0, keepdims=True)
        return loss + jnp.sum(cosine, axis=0, keepdims=True)

    def backward(j, _):
        cut = pl.ds(pl.multiple_of(j * wide, wide), wide)
        back = lax.dot_general(cot[...], wout[cut, :], (((1,), (1,)), ((), ())), preferred_element_type=f32)
        got = (back * dsilu[:, cut]).astype(bf16)
        dpre[:, cut] = got
        dpre_t[cut, :] = got.T
        brow[:, cut] = jnp.sum(got.astype(f32), axis=0, keepdims=True)
        return 0

    step = 384 if width % 384 == 0 else 128

    def to_rows(j, _):
        cut = pl.ds(pl.multiple_of(j * step, step), step)
        ghid[:, cut] = jnp.dot(dpre[...], win[:, cut], preferred_element_type=f32).astype(bf16)
        return 0

    def produce(s):
        order, split, which, lo_col, hi_col = streams[s]
        lhs, rhs = (act_t, cot) if which == 0 else (dpre_t, rows)
        hi, lo = split[0]
        keep, send, recv = bufs[s][:3]
        own = mine(order[0])

        def term(h, bit):
            at = pl.multiple_of((h * 2 + bit) * (lo * blk), lo * blk)
            got = jnp.dot(lhs[pl.ds(at, lo * blk), :], rhs[:, lo_col:hi_col], preferred_element_type=f32)
            return got.reshape(lo, blk, hi_col - lo_col)

        def to_send(h, _):
            send[pl.ds(h * lo, lo)] = term(h, 1 - own).astype(bf16)
            return 0

        def to_keep(h, _):
            keep[pl.ds(h * lo, lo)] = term(h, own)
            return 0

        lax.fori_loop(0, hi, to_send, 0)
        copy(s, 0).start()
        lax.fori_loop(0, hi, to_keep, 0)

    def advance(s, k):
        order, split = streams[s][:2]
        hi, lo = split[k]
        keep, recv0, send = bufs[s][0], bufs[s][2 * k], bufs[s][2 * k + 1]
        own = mine(order[k])
        copy(s, k - 1).wait_recv()

        def total(i, bit):
            at = (lax.div(i, lo) * 2 + bit) * lo + lax.rem(i, lo)
            return keep[at] + recv0[at].astype(f32)

        def to_send(i, _):
            send[i] = total(i, 1 - own).astype(bf16)
            return 0

        def to_keep(i, _):
            keep[i] = total(i, own)
            return 0

        lax.fori_loop(0, hi * lo, to_send, 0)
        copy(s, k).start()
        lax.fori_loop(0, hi * lo, to_keep, 0)

    blocks = dp * feat

    def small_step(k):
        if k == 0:
            small_send[0] = jnp.zeros(small_send.shape[1:], f32)
            for j in range(blocks):
                small_send[0, j : j + 1, 0:blk] = brow[:, j * blk : (j + 1) * blk]
            for j in range(channels // 128):
                small_send[0, blocks + j : blocks + j + 1, :] = bacc[:, j * 128 : (j + 1) * 128]
            last = blocks + channels // 128
            small_send[0, last : last + 1, :] = jnp.broadcast_to(lacc[...], (1, 128))
        else:
            small_copy(k - 1).wait_recv()
            small_send[k] = small_send[k - 1] + small_recv[k - 1]
        small_copy(k).start()

    def finish(s):
        which, lo_col, hi_col = streams[s][2:]
        copy(s, stages - 1).wait_recv()
        target = gout if which == 0 else gin
        target[:, lo_col:hi_col] = bufs[s][0][0] + bufs[s][2 * stages][0].astype(f32)

    loads[0].wait()
    loads[1].wait()
    lax.fori_loop(0, hidden // wide, first_map, 0)
    loads[2].wait()
    lax.fori_loop(0, channels // wide, last_map, 0)
    bacc[...] = jnp.zeros_like(bacc)
    loads[3].wait()
    for r in range(1, feat):
        tea_copy(r).wait_recv()
    lacc[...] = lax.fori_loop(0, tokens // some, cotangent, jnp.zeros((1, 1), f32))

    for t in range(stages + len(groups)):
        for g, group in enumerate(groups):
            k = t - g
            for s in group:
                if k == 0:
                    produce(s)
                elif 0 < k < stages:
                    advance(s, k)
                elif k == stages:
                    finish(s)
            if t == 1 and g == 0:
                lax.fori_loop(0, hidden // wide, backward, 0)
            if g == 1 and 0 <= k < stages:
                small_step(k)
        if t == 2:
            lax.fori_loop(0, width // step, to_rows, 0)
    small_copy(stages - 1).wait_recv()
    gsmall[...] = small_send[stages - 1] + small_recv[stages - 1]
    for r in range(1, feat):
        tea_copy(r).wait_send()
    for k in range(stages):
        for s in range(len(streams)):
            copy(s, k).wait_send()
        small_copy(k).wait_send()


def place_kernel(scale, blocks, gout, gin, gsmall, ghid, out_in, out_bias_in, out_out, out_bias_out, out_hid, out_loss):
    me = lax.axis_index("dp") * lax.axis_size("feat") + lax.axis_index("feat")
    out_in[...] = gin[...] * scale
    out_out[...] = gout[...] * scale
    out_hid[...] = ghid[...]
    blk = out_bias_in.shape[1]
    out_bias_in[...] = gsmall[pl.ds(me, 1), 0:blk] * scale
    rows = out_bias_out.shape[0]
    out_bias_out[...] = gsmall[blocks : blocks + rows, :] * scale
    out_loss[...] = gsmall[blocks + rows : blocks + rows + 1, 0:1] * (-scale)


def units(size, shares):
    total, parts, edge = size // 128, [], 0
    for i in range(len(shares)):
        upto = round(total * sum(shares[: i + 1]) / sum(shares))
        parts.append((edge * 128, upto * 128 if i < len(shares) - 1 else size))
        edge = upto
    return parts


def on_device(hidden_states, teacher, proj_in, bias_in, proj_out, bias_out):
    samples, seq, width = hidden_states.shape
    hidden, channels = proj_out.shape
    tokens = samples * seq
    rows = hidden_states.reshape(tokens, width)
    dp, feat = lax.axis_size("dp"), lax.axis_size("feat")
    scale = 1.0 / float(tokens * dp * feat)
    blocks = dp * feat
    blk = hidden // blocks
    part = channels // feat
    orders = stage_orders(dp, feat)
    stages = log2(dp) + log2(feat)
    streams, bufs, groups = [], [], [[], [], []]
    layout = [
        (0, channels, (3, 3, 2), (0, 0, 0), (0, 1, 2)),
        (1, width, (3, 3, 2, 1), (1, 1, 2, 2), (0, 1, 0, 1)),
    ]
    for which, size, shares, group_of, order_of in layout:
        for (lo, hi), group, kind in zip(units(size, shares), group_of, order_of):
            order = orders[kind]
            split = splits(order, dp, feat)
            groups[group].append(len(streams))
            streams.append((order, split, which, lo, hi))
            bufs.append(pltpu.VMEM((split[0][0] * split[0][1], blk, hi - lo), f32))
            for above, below in split:
                bufs += [pltpu.VMEM((above * below, blk, hi - lo), bf16)] * 2
    vmem = pl.BlockSpec(memory_space=pltpu.VMEM)
    hbm = pl.BlockSpec(memory_space=pl.ANY)
    small_rows = -(-(blocks + channels // 128 + 1) // 8) * 8
    gout, gin, gsmall, ghid = pl.pallas_call(
        functools.partial(train_kernel, (groups, streams, dp, feat, blk)),
        out_shape=(
            jax.ShapeDtypeStruct((blk, channels), f32),
            jax.ShapeDtypeStruct((blk, width), f32),
            jax.ShapeDtypeStruct((small_rows, 128), f32),
            jax.ShapeDtypeStruct((tokens, width), bf16),
        ),
        in_specs=[hbm] * 4 + [vmem] * 2,
        out_specs=(vmem,) * 4,
        scratch_shapes=[
            pltpu.VMEM((tokens, width), bf16),
            pltpu.VMEM((hidden, width), bf16),
            pltpu.VMEM((hidden, channels), bf16),
            pltpu.VMEM((feat, samples, seq, part), bf16),
            pltpu.VMEM((tokens, hidden), bf16),
            pltpu.VMEM((hidden, tokens), bf16),
            pltpu.VMEM((hidden, tokens), bf16),
            pltpu.VMEM((tokens, hidden), f32),
            pltpu.VMEM((tokens, channels), f32),
            pltpu.VMEM((tokens, channels), bf16),
            pltpu.VMEM((1, hidden), f32),
            pltpu.VMEM((1, channels), f32),
            pltpu.VMEM((1, 1), f32),
        ]
        + bufs
        + [
            pltpu.VMEM((stages, small_rows, 128), f32),
            pltpu.VMEM((stages, small_rows, 128), f32),
            pltpu.SemaphoreType.DMA((len(streams) + 1, stages)),
            pltpu.SemaphoreType.DMA((len(streams) + 1, stages)),
            pltpu.SemaphoreType.DMA((feat - 1,)),
            pltpu.SemaphoreType.DMA((feat - 1,)),
            pltpu.SemaphoreType.DMA((4,)),
        ],
        compiler_params=pltpu.CompilerParams(collective_id=0, has_side_effects=True, vmem_limit_bytes=63 * 1024 * 1024),
        name="train",
    )(teacher, rows, proj_in, proj_out, bias_in.reshape(1, hidden), bias_out.reshape(1, channels))
    grad_in, grad_bias_in, grad_out, grad_bias_out, grad_hidden, loss = pl.pallas_call(
        functools.partial(place_kernel, scale, blocks),
        out_shape=(
            jax.ShapeDtypeStruct((blk, width), f32),
            jax.ShapeDtypeStruct((1, blk), f32),
            jax.ShapeDtypeStruct((blk, channels), f32),
            jax.ShapeDtypeStruct((channels // 128, 128), f32),
            jax.ShapeDtypeStruct((tokens, width), bf16),
            jax.ShapeDtypeStruct((1, 1), f32),
        ),
        in_specs=[vmem] * 4,
        out_specs=(vmem,) * 6,
        name="place",
    )(gout, gin, gsmall, ghid)
    return (
        grad_in,
        grad_bias_in.reshape(blk),
        grad_out,
        grad_bias_out.reshape(channels),
        grad_hidden.reshape(samples, seq, width),
        loss.reshape(()),
    )


def solution(mesh):
    return jax.shard_map(
        on_device,
        mesh=mesh,
        in_specs=(P(("dp", "feat"), None, None), P("dp", None, "feat"), P(), P(), P(), P()),
        out_specs=(
            P(("dp", "feat"), None),
            P(("dp", "feat")),
            P(("dp", "feat"), None),
            P(),
            P(("dp", "feat"), None, None),
            P(),
        ),
        check_vma=False,
    )
```

time: 129 us -> 92.7 us (0.72)
  Pallas kernels: 68.9 us -> 91.8 us
  matrix products: 21.4 us -> 0 us
  waiting for transfers between devices: 17.1 us -> 0 us
  local copies, waits for them, and re-layouts: 10.8 us -> 0 us
  starting transfers between devices: 6.36 us -> 0 us
  between operations: 2.58 us -> 0.64 us
  other arithmetic: 1.53 us -> 0 us
    pallas_call x1 -> x2, Pallas kernels: 68.9 us -> 91.8 us  [the longest x1 89.1 us: on_device(): pl.pallas_call(functools.partial(train_kernel, (groups, streams, dp, feat...]
    dot_general x4 -> x0, matrix products: 21.4 us -> none  [the longest x1 8.62 us: on_device(): lax.dot_general(rows, proj_in, (((1,), (1,)), ((), ())), preferred_elemen...]
    all_to_all x1 -> x0, waiting for transfers between devices: 17.1 us -> none  [on_device(): lax.all_to_all(teacher, 'feat', split_axis=0, concat_axis=2, tiled=True)]
    all_to_all x1 -> x0, starting transfers between devices: 6.36 us -> none  [on_device(): lax.all_to_all(teacher, 'feat', split_axis=0, concat_axis=2, tiled=True)]
    unnamed x20 -> x0, local copies, waits for them, and re-layouts: 4.96 us -> none
    slice x2 -> x0, local copies, waits for them, and re-layouts: 2.45 us -> none  [the longest x1 1.27 us: on_device(): sums[hidden:hidden + channels]]
    reduce_sum x4 -> x0, other arithmetic: 1.51 us -> none  [the longest x1 0.62 us: on_device(): jnp.sum(cosine)[None]]
    concatenate x1 -> x0, local copies, waits for them, and re-layouts: 1.32 us -> none  [on_device(): jnp.concatenate(parts + [jnp.zeros((padded - count,), f32)])]
  transfers between devices with their start and end apart: 1 -> 0, of which waited for: 1 -> 0; matrix products, arithmetic and copies ran while one was open for 7% -> 0% of each run, Pallas kernels for 0% -> 0%
where the time goes in v2:
time: 92.7 us; the launch traced here: 92.5 us
  Pallas kernels  91.8 us (99%)
    pallas_call x1, Pallas kernels, on_device(): pl.pallas_call(functools.partial(train_kernel, (groups, streams, dp, feat...  89.1 us
    pallas_call x1, Pallas kernels, on_device(): pl.pallas_call(functools.partial(place_kernel, scale, blocks), out_shape=...  2.71 us

profile of v2, /device:TPU:0, one launch (start us, length us, event | category | flops | bytes accessed | tf_op | source)
XLA Modules:
  0.0 92.5 jit_solution(11275130654224416672)
XLA Ops:
  0.6 89.1 %train.1 = (f32[64,1024]{1,0:T(8,128)}, f32[64,1152]{1,0:T(8,128)}, f32[48,128]{1,0:T(8,128)}, bf16[512,1152]{1,0:T(8,128)(2,1)}) custom-call(bf16[8,256,256]{2,1,0:T(8,128)(2,1)} %teacher_hbm.1, bf16[512,1152]{1,0:T(8,128)(2,1)} %bitcast.7, bf16[2048,1152]{1,0:T(8,128)(2,1)} %win_hbm.1, bf16[2048,1024]{1,0:T(8,128)(2,1)} %wout_hbm.1, f32[1,2048]{1,0:T(1,128)} %bitcast.8, ...), custom_call_target="tpu_custom_call" | custom-call | tf_op jit(solution)/shard_map/train/pallas_call | solution.py:322
  89.7 2.7 %place.1 = (f32[64,1152]{1,0:T(8,128)}, f32[1,64]{1,0:T(1,128)}, f32[64,1024]{1,0:T(8,128)}, f32[8,128]{1,0:T(8,128)}, bf16[512,1152]{1,0:T(8,128)(2,1)}, /*index=5*/f32[1,1]{1,0:T(1,128)}) custom-call(f32[64,1024]{1,0:T(8,128)} %get-tuple-element.16.gout, f32[64,1152]{1,0:T(8,128)} %get-tuple-element.17.gin, f32[48,128]{1,0:T(8,128)} %get-tuple-element.18.gsmall, ...), custom_call_target="tpu_custom_call" | custom-call | tf_op jit(solution)/shard_map/place/pallas_call | solution.py:360

commit v3 on v2

--- a/solution.py
+++ b/solution.py
@@ -77,16 +77,17 @@
         load.start()
     pl.semaphore_wait(barrier, log2(dp) + feat - 1)
 
-    def tea_copy(r):
+    def tea_copy(sample, r):
         peer = lax.rem(place["feat"] + r, feat)
         return pltpu.make_async_remote_copy(
-            src_ref=teacher_hbm.at[pl.ds(peer * samples, samples)], dst_ref=tea.at[place["feat"]],
-            send_sem=tea_send.at[r - 1], recv_sem=tea_recv.at[r - 1],
+            src_ref=teacher_hbm.at[peer * samples + sample], dst_ref=tea.at[place["feat"], sample],
+            send_sem=tea_send.at[sample, r - 1], recv_sem=tea_recv.at[sample, r - 1],
             device_id={"feat": peer}, device_id_type=MESH,
         )
 
-    for r in range(1, feat):
-        tea_copy(r).start()
+    for sample in range(samples):
+        for r in range(1, feat):
+            tea_copy(sample, r).start()
 
     def copy(s, k):
         send, recv = bufs[s][1 + 2 * k : 3 + 2 * k]
@@ -122,10 +123,9 @@
 
     some = 64
 
-    def cotangent(i, loss):
-        at = pl.ds(pl.multiple_of(i * some, some), some)
-        sample, off = lax.div(i, seq // some), lax.rem(i, seq // some)
-        inner = pl.ds(pl.multiple_of(off * some, some), some)
+    def cotangent(sample, i, loss):
+        at = pl.ds(pl.multiple_of(sample * seq + i * some, some), some)
+        inner = pl.ds(pl.multiple_of(i * some, some), some)
         zz = jnp.zeros((some, 1), f32)
         yy, zy = zz, zz
         for c in range(feat):
@@ -147,14 +147,18 @@
             bacc[:, c * part : (c + 1) * part] += jnp.sum(got.astype(f32), axis=0, keepdims=True)
         return loss + jnp.sum(cosine, axis=0, keepdims=True)
 
-    def backward(j, _):
+    def backward(sample, j, _):
         cut = pl.ds(pl.multiple_of(j * wide, wide), wide)
-        back = lax.dot_general(cot[...], wout[cut, :], (((1,), (1,)), ((), ())), preferred_element_type=f32)
-        got = (back * dsilu[:, cut]).astype(bf16)
-        dpre[:, cut] = got
-        dpre_t[cut, :] = got.T
-        brow[:, cut] = jnp.sum(got.astype(f32), axis=0, keepdims=True)
+        own = slice(sample * seq, (sample + 1) * seq)
+        back = lax.dot_general(cot[own, :], wout[cut, :], (((1,), (1,)), ((), ())), preferred_element_type=f32)
+        got = (back * dsilu[own, cut]).astype(bf16)
+        dpre[own, cut] = got
+        dpre_t[cut, own] = got.T
+        brow[:, cut] += jnp.sum(got.astype(f32), axis=0, keepdims=True)
         return 0
+
+    def back_through(sample):
+        lax.fori_loop(0, hidden // wide, functools.partial(backward, sample), 0)
 
     step = 384 if width % 384 == 0 else 128
 
@@ -163,7 +167,7 @@
         ghid[:, cut] = jnp.dot(dpre[...], win[:, cut], preferred_element_type=f32).astype(bf16)
         return 0
 
-    def produce(s):
+    def produce(s, sends):
         order, split, which, lo_col, hi_col = streams[s]
         lhs, rhs = (act_t, cot) if which == 0 else (dpre_t, rows)
         hi, lo = split[0]
@@ -183,9 +187,17 @@
             keep[pl.ds(h * lo, lo)] = term(h, own)
             return 0
 
-        lax.fori_loop(0, hi, to_send, 0)
-        copy(s, 0).start()
-        lax.fori_loop(0, hi, to_keep, 0)
+        if sends:
+            lax.fori_loop(0, hi, to_send, 0)
+            copy(s, 0).start()
+        else:
+            lax.fori_loop(0, hi, to_keep, 0)
+
+    def produce_all(group):
+        for s in group:
+            produce(s, True)
+        for s in group:
+            produce(s, False)
 
     def advance(s, k):
         order, split = streams[s][:2]
@@ -238,31 +250,53 @@
     loads[2].wait()
     lax.fori_loop(0, channels // wide, last_map, 0)
     bacc[...] = jnp.zeros_like(bacc)
+    brow[...] = jnp.zeros_like(brow)
     loads[3].wait()
-    for r in range(1, feat):
-        tea_copy(r).wait_recv()
-    lacc[...] = lax.fori_loop(0, tokens // some, cotangent, jnp.zeros((1, 1), f32))
-
-    for t in range(stages + len(groups)):
-        for g, group in enumerate(groups):
+    loss = jnp.zeros((1, 1), f32)
+    for sample in range(samples):
+        for r in range(1, feat):
+            tea_copy(sample, r).wait_recv()
+        loss = lax.fori_loop(0, seq // some, functools.partial(cotangent, sample), loss)
+        if sample < samples - 1:
+            back_through(sample)
+    lacc[...] = loss
+
+    first, second, third = groups
+    one, two, other = first
+    produce(one, True)
+    produce(two, True)
+    produce(one, False)
+    produce(other, True)
+    advance(one, 1)
+    produce(two, False)
+    advance(two, 1)
+    produce(other, False)
+    advance(other, 1)
+    back_through(samples - 1)
+    produce_all(second)
+    small_step(0)
+    for s in second:
+        advance(s, 1)
+    small_step(1)
+    produce_all(third)
+    for s in first:
+        advance(s, 2)
+    lax.fori_loop(0, width // step, to_rows, 0)
+    for t in range(3, stages + 3):
+        for g in (2, 1, 0):
             k = t - g
-            for s in group:
-                if k == 0:
-                    produce(s)
-                elif 0 < k < stages:
+            for s in groups[g]:
+                if k < stages:
                     advance(s, k)
                 elif k == stages:
                     finish(s)
-            if t == 1 and g == 0:
-                lax.fori_loop(0, hidden // wide, backward, 0)
-            if g == 1 and 0 <= k < stages:
+            if g == 1 and k < stages:
                 small_step(k)
-        if t == 2:
-            lax.fori_loop(0, width // step, to_rows, 0)
     small_copy(stages - 1).wait_recv()
     gsmall[...] = small_send[stages - 1] + small_recv[stages - 1]
-    for r in range(1, feat):
-        tea_copy(r).wait_send()
+    for sample in range(samples):
+        for r in range(1, feat):
+            tea_copy(sample, r).wait_send()
     for k in range(stages):
         for s in range(len(streams)):
             copy(s, k).wait_send()
@@ -350,8 +384,8 @@
             pltpu.VMEM((stages, small_rows, 128), f32),
             pltpu.SemaphoreType.DMA((len(streams) + 1, stages)),
             pltpu.SemaphoreType.DMA((len(streams) + 1, stages)),
-            pltpu.SemaphoreType.DMA((feat - 1,)),
-            pltpu.SemaphoreType.DMA((feat - 1,)),
+            pltpu.SemaphoreType.DMA((samples, feat - 1)),
+            pltpu.SemaphoreType.DMA((samples, feat - 1)),
             pltpu.SemaphoreType.DMA((4,)),
         ],
         compiler_params=pltpu.CompilerParams(collective_id=0, has_side_effects=True, vmem_limit_bytes=63 * 1024 * 1024),

time: 92.7 us -> 90.4 us (0.975)
  Pallas kernels: 91.8 us -> 89.5 us
    pallas_call x1, Pallas kernels: 89.1 us -> 86.8 us  [on_device(): pl.pallas_call(functools.partial(train_kernel, (groups, streams, dp, feat...]
where the time goes in v3:
time: 90.4 us; the launch traced here: 90.1 us
  Pallas kernels  89.5 us (99%)
    pallas_call x1, Pallas kernels, on_device(): pl.pallas_call(functools.partial(train_kernel, (groups, streams, dp, feat...  86.8 us
    pallas_call x1, Pallas kernels, on_device(): pl.pallas_call(functools.partial(place_kernel, scale, blocks), out_shape=...  2.71 us

profile of v3, /device:TPU:0, one launch (start us, length us, event | category | flops | bytes accessed | tf_op | source)
XLA Modules:
  0.0 90.1 jit_solution(2921806431950426536)
XLA Ops:
  0.6 86.8 %train.1 = (f32[64,1024]{1,0:T(8,128)}, f32[64,1152]{1,0:T(8,128)}, f32[48,128]{1,0:T(8,128)}, bf16[512,1152]{1,0:T(8,128)(2,1)}) custom-call(bf16[8,256,256]{2,1,0:T(8,128)(2,1)} %teacher_hbm.1, bf16[512,1152]{1,0:T(8,128)(2,1)} %bitcast.7, bf16[2048,1152]{1,0:T(8,128)(2,1)} %win_hbm.1, bf16[2048,1024]{1,0:T(8,128)(2,1)} %wout_hbm.1, f32[1,2048]{1,0:T(1,128)} %bitcast.8, ...), custom_call_target="tpu_custom_call" | custom-call | tf_op jit(solution)/shard_map/train/pallas_call | solution.py:356
  87.4 2.7 %place.1 = (f32[64,1152]{1,0:T(8,128)}, f32[1,64]{1,0:T(1,128)}, f32[64,1024]{1,0:T(8,128)}, f32[8,128]{1,0:T(8,128)}, bf16[512,1152]{1,0:T(8,128)(2,1)}, /*index=5*/f32[1,1]{1,0:T(1,128)}) custom-call(f32[64,1024]{1,0:T(8,128)} %get-tuple-element.16.gout, f32[64,1152]{1,0:T(8,128)} %get-tuple-element.17.gin, f32[48,128]{1,0:T(8,128)} %get-tuple-element.18.gsmall, ...), custom_call_target="tpu_custom_call" | custom-call | tf_op jit(solution)/shard_map/place/pallas_call | solution.py:394
